TPU v7x, 16 devices: a whole 2x2x2 slice. The times are simulated.
16 devices in a mesh: stage: 2 (over z), expert: 8 (over y, x, core).
Axes of the slice: x: 2, y: 2, z: 2, core: 2. Of those that a mesh axis runs over, the one named last changes fastest.
Arguments:
- w_gate: bfloat16 [2, 16, 2048, 1024], P('stage', 'expert')
- w_up: bfloat16 [2, 16, 2048, 1024], P('stage', 'expert')
- w_down: bfloat16 [2, 16, 1024, 2048], P('stage', 'expert')
- x: bfloat16 [4096, 2048], P(('stage', 'expert'))
- expert_ids: int32 [2, 4096, 8], P(None, ('stage', 'expert'))
- gates: float32 [2, 4096, 8], P(None, ('stage', 'expert'))
Outputs:
- output 1: bfloat16 [2, 16, 2048, 2048], P(None, ('stage', 'expert'))
- output 2: bfloat16 [2, 16, 1024, 2048], P(None, ('stage', 'expert'))
- output 3: float32 [2, 4096, 2048], P(None, ('stage', 'expert'))
All inputs are finite; a program needn't handle non-finite values.
Results may differ from a plain program's by a relative error of at most 0.001.
Values are sent between devices in bfloat16 or wider.
A program may use at most 1 GiB of HBM per device.

v0:
```python
import jax
import jax.numpy as jnp
from jax import lax
from jax.sharding import PartitionSpec as P

NORM_EPS = 1e-6
FLAT = ("stage", "expert")


def norm_rows(hidden):
    return (hidden * lax.rsqrt(jnp.mean(hidden * hidden, axis=-1, keepdims=True) + NORM_EPS)).astype(jnp.bfloat16)


def slot_table(layer_ids, n_experts, capacity):
    flat_ids = layer_ids.reshape(-1)
    onehot = (flat_ids[:, None] == jnp.arange(n_experts)[None, :]).astype(jnp.int32)
    pair_rank = jnp.sum(onehot * jnp.cumsum(onehot, axis=0), axis=-1) - 1
    return flat_ids * capacity + pair_rank


def moe_layer(hidden, layer_w13, layer_down, layer_ids, layer_mix, capacity, dev_count):
    tok_dev, model_width = hidden.shape
    top_k = layer_ids.shape[-1]
    exp_dev = layer_w13.shape[0]
    expert_width = layer_down.shape[1]
    n_experts = exp_dev * dev_count
    normed = norm_rows(hidden)
    slot_pos = slot_table(layer_ids, n_experts, capacity)
    pair_tok = jnp.arange(tok_dev * top_k, dtype=jnp.int32) // top_k
    source_row = jnp.zeros((n_experts * capacity,), jnp.int32).at[slot_pos].set(pair_tok)
    outbound = jnp.take(normed, source_row, axis=0).reshape(dev_count, exp_dev, capacity, model_width)
    inbound = lax.all_to_all(outbound, FLAT, 0, 0, tiled=True)
    projected = jnp.einsum("nxcd,xdg->nxcg", inbound, layer_w13, preferred_element_type=jnp.float32)
    activated = (jax.nn.silu(projected[..., :expert_width]) * projected[..., expert_width:]).astype(jnp.bfloat16)
    expert_out = jnp.einsum("nxcf,xfd->nxcd", activated, layer_down, preferred_element_type=jnp.float32).astype(jnp.bfloat16)
    returned = lax.all_to_all(expert_out, FLAT, 0, 0, tiled=True)
    picked = jnp.take(returned.reshape(n_experts * capacity, model_width), slot_pos, axis=0)
    picked = picked.reshape(tok_dev, top_k, model_width).astype(jnp.float32)
    return hidden + jnp.sum(layer_mix[..., None] * picked, axis=1)


def hand_over(gate_loc, up_loc, down_loc, n_stage, n_group):
    stage_idx = lax.axis_index("stage")
    flat_idx = stage_idx * n_group + lax.axis_index("expert")
    lay_stage = gate_loc.shape[0]
    exp_dev = gate_loc.shape[1] // n_stage
    fused_loc = jnp.concatenate([gate_loc, up_loc], axis=-1)
    fused_new = jnp.zeros((lay_stage * n_stage, exp_dev) + fused_loc.shape[2:], fused_loc.dtype)
    down_new = jnp.zeros((lay_stage * n_stage, exp_dev) + down_loc.shape[2:], down_loc.dtype)
    for round_idx in range(n_stage):
        pair_list = [(src_stage * n_group + src_group, src_group * n_stage + (src_stage + round_idx) % n_stage) for src_stage in range(n_stage) for src_group in range(n_group)]
        piece_idx = (stage_idx + round_idx) % n_stage
        fused_in = lax.ppermute(lax.dynamic_slice_in_dim(fused_loc, piece_idx * exp_dev, exp_dev, axis=1), FLAT, pair_list)
        down_in = lax.ppermute(lax.dynamic_slice_in_dim(down_loc, piece_idx * exp_dev, exp_dev, axis=1), FLAT, pair_list)
        from_stage = (flat_idx % n_stage - round_idx) % n_stage
        fused_new = lax.dynamic_update_slice_in_dim(fused_new, fused_in, from_stage * lay_stage, axis=0)
        down_new = lax.dynamic_update_slice_in_dim(down_new, down_in, from_stage * lay_stage, axis=0)
    return fused_new, down_new


def solution(mesh):
    n_stage = mesh.shape["stage"]
    n_group = mesh.shape["expert"]
    dev_count = n_stage * n_group

    def per_device(gate_loc, up_loc, down_loc, x_loc, ids_loc, mix_loc):
        fused_new, down_new = hand_over(gate_loc, up_loc, down_loc, n_stage, n_group)
        n_experts = fused_new.shape[1] * dev_count
        capacity = 3 * x_loc.shape[0] * ids_loc.shape[-1] // (2 * n_experts)
        hidden = x_loc.astype(jnp.float32)
        layer_outs = []
        for layer_idx in range(fused_new.shape[0]):
            hidden = moe_layer(hidden, fused_new[layer_idx], down_new[layer_idx], ids_loc[layer_idx], mix_loc[layer_idx], capacity, dev_count)
            layer_outs.append(hidden)
        return fused_new, down_new, jnp.stack(layer_outs)

    weight_spec = P("stage", "expert")
    token_spec = P(None, FLAT)
    return jax.shard_map(per_device, mesh=mesh, in_specs=(weight_spec, weight_spec, weight_spec, P(FLAT), token_spec, token_spec), out_specs=(token_spec, token_spec, token_spec), check_vma=False)
```

profile of v0, /device:TPU:9, one launch (start us, length us, event | category | flops | bytes accessed | tf_op | source)
XLA Modules:
  0.0 1175.0 jit_solution(7128430490550076591)
XLA Ops:
  0.6 1.3 fusion.38
  2.6 4.5 reduce-window.14
  7.2 0.4 slice_reduce_fusion.1
  7.9 0.6 broadcast_clamp_fusion.1
  8.6 8.1 scatter_custom_fusion
  16.7 1.5 fusion.18
  18.2 1.5 fusion.19
  19.7 15.7 %gather_fusion = bf16[3072,2048]{1,0:T(8,128)(2,1)} fusion(bf16[256,2048]{1,0:T(8,128)(2,1)S(1)} %fusion.19, s32[3072]{0:T(1024)S(1)} %fusion.27), kind=kCustom, calls=%fused_computation.clone | custom fusion | bytes 25178112 | tf_op jit(solution)/shard_map/jit(_take)/gather | solution.py:31
  35.4 11.1 broadcast_select_fusion.1
  46.5 4.2 all-to-all-start
  50.7 7.8 constant_dynamic-update-slice_fusion.1
  58.5 7.9 constant_dynamic-update-slice_fusion
  66.4 12.1 %constant_dynamic-slice_fusion.2 = (bf16[1,1,2048,2048]{3,2,1,0:T(8,128)(2,1)}, bf16[1,1,2048,2048]{3,2,1,0:T(8,128)(2,1)}) fusion(bf16[1,2,2048,2048]{3,2,1,0:T(8,128)(2,1)} %constant_dynamic-update-slice_fusion, s32[]{:T(128)S(6)} %select_n.88, s32[]{:T(128)S(6)} %select_n.83), kind=kLoop, calls=%fused_computation.94 | loop fusion | bytes 33554440 | tf_op jit(solution)/shard_map/dynamic_slice | solution.py:53
  78.5 3.1 collective-permute-start
  81.6 1.8 collective-permute-start.1
  83.4 4.2 constant_dynamic-slice_fusion
  87.6 3.3 collective-permute-start.2
  91.0 1.5 collective-permute-start.3
  92.5 339.2 %collective-permute-done.2 = bf16[1,1,1024,2048]{3,2,1,0:T(8,128)(2,1)} collective-permute-done((bf16[1,1,1024,2048]{3,2,1,0:T(8,128)(2,1)}, bf16[1,1,1024,2048]{3,2,1,0:T(8,128)(2,1)}, u32[]{:S(2)}, u32[]{:S(2)}) %collective-permute-start.2) | collective-permute-done | bytes 4194336 | tf_op jit(solution)/shard_map/ppermute | solution.py:54
  431.7 4.5 broadcast_in_dim.31
  436.1 4.8 constant_dynamic-update-slice_fusion.3
  440.9 35.7 %collective-permute-done.3 = bf16[1,1,1024,2048]{3,2,1,0:T(8,128)(2,1)} collective-permute-done((bf16[1,1,1024,2048]{3,2,1,0:T(8,128)(2,1)}, bf16[1,1,1024,2048]{3,2,1,0:T(8,128)(2,1)}, u32[]{:S(2)}, u32[]{:S(2)}) %collective-permute-start.3) | collective-permute-done | bytes 4194336 | tf_op jit(solution)/shard_map/ppermute | solution.py:54
  476.6 4.8 constant_dynamic-update-slice_fusion.2
  481.4 6.1 broadcast_in_dim.30
  487.5 8.4 constant_dynamic-update-slice_fusion.5
  496.0 8.4 constant_dynamic-update-slice_fusion.4
  504.4 33.9 %fusion.8 = f32[16,1,192,2048]{3,2,0,1:T(8,128)} fusion(bf16[16,1,192,2048]{3,2,1,0:T(8,128)(2,1)} %all-to-all-done, bf16[2,1,2048,2048]{3,2,1,0:T(8,128)(2,1)} %constant_dynamic-update-slice_fusion.4), kind=kOutput, calls=%fused_computation.22 | convolution fusion | flops 25769803776 | bytes 46137344 | tf_op jit(solution)/shard_map/nxcd,xdg->nxcg/dot_general | solution.py:33
  538.3 21.0 %convert_bitcast_fusion.1 = bf16[16,1,192,2048]{3,2,1,0:T(8,128)(2,1)} fusion(f32[16,1,192,2048]{3,2,0,1:T(8,128)} %fusion.8, bf16[2,1,1024,2048]{3,2,1,0:T(8,128)(2,1)} %constant_dynamic-update-slice_fusion.2), kind=kOutput, calls=%fused_computation.19 | convolution fusion | flops 12910067712 | bytes 41943040 | tf_op jit(solution)/shard_map/nxcf,xfd->nxcd/dot_general | solution.py:35
  559.3 4.0 all-to-all-start.1
  563.7 0.6 slice_bitcast_fusion.8
  564.7 4.5 reduce-window.16
  570.0 0.6 broadcast_clamp_fusion
  570.7 8.2 scatter_custom_fusion.1
  579.0 140.6 %all-to-all-done.1 = bf16[16,1,192,2048]{3,2,1,0:T(8,128)(2,1)} async-done(((bf16[16,1,192,2048]{3,2,1,0:T(8,128)(2,1)}), bf16[16,1,192,2048]{3,2,1,0:T(8,128)(2,1)}, u32[]{:S(2)}, u32[]{:S(2)}) %all-to-all-start.1) | async-done | bytes 12582944 | tf_op jit(solution)/shard_map/all_to_all | solution.py:36
  719.5 22.5 %gather_fusion.1 = bf16[2048,2048]{1,0:T(8,128)(2,1)} fusion(bf16[3072,2048]{1,0:T(8,128)(2,1)} %bitcast.18, s32[2048]{0:T(1024)S(1)} %copy-done.13), kind=kCustom, calls=%fused_computation.1.clone | custom fusion | bytes 16785408 | tf_op jit(solution)/shard_map/jit(_take)/gather | solution.py:37
  742.1 9.8 fusion.1
  751.9 1.8 fusion.20
  754.1 15.9 %gather_fusion.2 = bf16[3072,2048]{1,0:T(8,128)(2,1)} fusion(bf16[256,2048]{1,0:T(8,128)(2,1)S(1)} %multiply_convert_fusion, s32[3072]{0:T(1024)S(1)} %fusion.28), kind=kCustom, calls=%fused_computation.2.clone | custom fusion | bytes 25178112 | tf_op jit(solution)/shard_map/jit(_take)/gather | solution.py:31
  770.0 7.0 broadcast_select_fusion
  777.0 145.7 %all_to_all.20 = bf16[16,1,192,2048]{3,2,1,0:T(8,128)(2,1)S(1)} all-to-all(bf16[16,1,192,2048]{3,2,1,0:T(8,128)(2,1)S(1)} %bitcast.111), channel_id=1, replica_groups=mesh['stage'=2,'expert'=8] {'stage','expert'}, dimensions={0} | all-to-all | bytes 25165824 | tf_op jit(solution)/shard_map/all_to_all | solution.py:32
  922.7 31.0 %fusion.11 = f32[16,1,192,2048]{3,2,0,1:T(8,128)} fusion(bf16[16,1,192,2048]{3,2,1,0:T(8,128)(2,1)S(1)} %all_to_all.20, bf16[2,1,2048,2048]{3,2,1,0:T(8,128)(2,1)} %constant_dynamic-update-slice_fusion.4), kind=kOutput, calls=%fused_computation.23 | convolution fusion | flops 25769803776 | bytes 46137344 | tf_op jit(solution)/shard_map/nxcd,xdg->nxcg/dot_general | solution.py:33
  953.7 20.8 %convert_bitcast_fusion = bf16[16,1,192,2048]{3,2,1,0:T(8,128)(2,1)} fusion(f32[16,1,192,2048]{3,2,0,1:T(8,128)} %fusion.11, bf16[2,1,1024,2048]{3,2,1,0:T(8,128)(2,1)} %constant_dynamic-update-slice_fusion.2), kind=kOutput, calls=%fused_computation.18 | convolution fusion | flops 12910067712 | bytes 41943040 | tf_op jit(solution)/shard_map/nxcf,xfd->nxcd/dot_general | solution.py:35
  974.5 8.4 all-to-all-start.3
  983.1 155.9 %all-to-all-done.3 = bf16[16,1,192,2048]{3,2,1,0:T(8,128)(2,1)} async-done(((bf16[16,1,192,2048]{3,2,1,0:T(8,128)(2,1)}), bf16[16,1,192,2048]{3,2,1,0:T(8,128)(2,1)}, u32[]{:S(2)}, u32[]{:S(2)}) %all-to-all-start.3) | async-done | bytes 12582944 | tf_op jit(solution)/shard_map/all_to_all | solution.py:36
  1139.0 22.5 %gather_fusion.3 = bf16[2048,2048]{1,0:T(8,128)(2,1)} fusion(bf16[3072,2048]{1,0:T(8,128)(2,1)} %bitcast.39, s32[2048]{0:T(1024)S(1)} %copy-done.14), kind=kCustom, calls=%fused_computation.3.clone | custom fusion | bytes 16785408 | tf_op jit(solution)/shard_map/jit(_take)/gather | solution.py:37
  1161.6 9.8 fusion
  1171.4 0.6 add_bitcast_fusion
  1172.1 2.5 pad_maximum_fusion
  (81 shorter events, 3.2 us)
Async XLA Ops:
  2.2 16.0 %copy-start.5 = (s32[2048]{0:T(1024)}, s32[2048]{0:T(1024)S(1)}, u32[]{:S(2)}) copy-start(s32[2048]{0:T(1024)S(1)} %eq.57) | copy-start | bytes 24580
  2.3 15.9 %copy-start.19 = (s32[2048]{0:T(1024)}, s32[2048]{0:T(1024)S(1)}, u32[]{:S(2)}) copy-start(s32[2048]{0:T(1024)S(1)} %add_select_fusion) | copy-start | bytes 24580
  7.9 0.6 copy-start.9
  46.5 457.9 %all-to-all-start = ((bf16[16,1,192,2048]{3,2,1,0:T(8,128)(2,1)}), bf16[16,1,192,2048]{3,2,1,0:T(8,128)(2,1)}, u32[]{:S(2)}, u32[]{:S(2)}) async-start(bf16[16,1,192,2048]{3,2,1,0:T(8,128)(2,1)} %bitcast.110), calls=%async_computation | async-start | bytes 25165824 | tf_op jit(solution)/shard_map/all_to_all | solution.py:32
  58.5 24.9 %slice-start = ((s8[8388608]{0:T(1024)(128)(4,1)}), s8[4194304]{0:T(1024)(128)(4,1)S(1)}, s32[]{:S(2)}) async-start(s8[8388608]{0:T(1024)(128)(4,1)} %bitcast.112), calls=%async_computation.4 | async-start | bytes 8388608
  66.4 17.0 %slice-start.1 = ((s8[8388608]{0:T(1024)(128)(4,1)}), s8[4194304]{0:T(1024)(128)(4,1)S(1)}, s32[]{:S(2)}) async-start(s8[8388608]{0:T(1024)(128)(4,1)} %bitcast.112), calls=%async_computation.5 | async-start | bytes 8388608
  78.5 402.9 %collective-permute-start = (bf16[1,1,2048,2048]{3,2,1,0:T(8,128)(2,1)}, bf16[1,1,2048,2048]{3,2,1,0:T(8,128)(2,1)}, u32[]{:S(2)}, u32[]{:S(2)}) collective-permute-start(bf16[1,1,2048,2048]{3,2,1,0:T(8,128)(2,1)} %get-tuple-element.6), channel_id=1, source_target_pairs={{0,0},{1,2},{2,4},{3,6},{4,8},{5,10},{6,12},{7,14},{8,1},{9,3},{10... | collective-permute-start | bytes 25165832 | tf_op jit(solution)/shard_map/ppermute | solution.py:53
  81.6 414.4 %collective-permute-start.1 = (bf16[1,1,2048,2048]{3,2,1,0:T(8,128)(2,1)}, bf16[1,1,2048,2048]{3,2,1,0:T(8,128)(2,1)}, u32[]{:S(2)}, u32[]{:S(2)}) collective-permute-start(bf16[1,1,2048,2048]{3,2,1,0:T(8,128)(2,1)} %get-tuple-element.5), channel_id=1, source_target_pairs={{0,1},{1,3},{2,5},{3,7},{4,9},{5,11},{6,13},{7,15},{8,0},{9,2},{10... | collective-permute-start | bytes 25165832 | tf_op jit(solution)/shard_map/ppermute | solution.py:53
  87.6 344.1 %collective-permute-start.2 = (bf16[1,1,1024,2048]{3,2,1,0:T(8,128)(2,1)}, bf16[1,1,1024,2048]{3,2,1,0:T(8,128)(2,1)}, u32[]{:S(2)}, u32[]{:S(2)}) collective-permute-start(bf16[1,1,1024,2048]{3,2,1,0:T(8,128)(2,1)} %get-tuple-element.8), channel_id=1, source_target_pairs={{0,0},{1,2},{2,4},{3,6},{4,8},{5,10},{6,12},{7,14},{8,1},{9,3},{10... | collective-permute-start | bytes 12582920 | tf_op jit(solution)/shard_map/ppermute | solution.py:54
  91.0 385.7 %collective-permute-start.3 = (bf16[1,1,1024,2048]{3,2,1,0:T(8,128)(2,1)}, bf16[1,1,1024,2048]{3,2,1,0:T(8,128)(2,1)}, u32[]{:S(2)}, u32[]{:S(2)}) collective-permute-start(bf16[1,1,1024,2048]{3,2,1,0:T(8,128)(2,1)} %get-tuple-element.7), channel_id=1, source_target_pairs={{0,1},{1,3},{2,5},{3,7},{4,9},{5,11},{6,13},{7,15},{8,0},{9,2},{10... | collective-permute-start | bytes 12582920 | tf_op jit(solution)/shard_map/ppermute | solution.py:54
  559.3 4.0 copy-start.16
  559.3 4.4 copy-start.18
  559.3 5.1 copy-start.15
  559.3 19.6 %copy-start.6 = (s32[2048]{0:T(1024)S(1)}, s32[2048]{0:T(1024)}, u32[]{:S(2)}) copy-start(s32[2048]{0:T(1024)} %copy-done.5) | copy-start | bytes 24580
  559.3 19.6 %copy-start.10 = (s32[2048]{0:T(1024)S(1)}, s32[2048]{0:T(1024)}, u32[]{:S(2)}) copy-start(s32[2048]{0:T(1024)} %copy-done.9) | copy-start | bytes 24580
  559.3 160.2 %copy-start.13 = (s32[2048]{0:T(1024)S(1)}, s32[2048]{0:T(1024)}, u32[]{:S(2)}) copy-start(s32[2048]{0:T(1024)} %get-tuple-element.19) | copy-start | bytes 24580
  559.3 160.2 %all-to-all-start.1 = ((bf16[16,1,192,2048]{3,2,1,0:T(8,128)(2,1)}), bf16[16,1,192,2048]{3,2,1,0:T(8,128)(2,1)}, u32[]{:S(2)}, u32[]{:S(2)}) async-start(bf16[16,1,192,2048]{3,2,1,0:T(8,128)(2,1)} %convert_bitcast_fusion.1), calls=%async_computation.1 | async-start | bytes 25165824 | tf_op jit(solution)/shard_map/all_to_all | solution.py:36
  563.6 178.5 %copy-start.7 = (s32[2048]{0:T(1024)}, s32[2048]{0:T(1024)S(1)}, u32[]{:S(2)}) copy-start(s32[2048]{0:T(1024)S(1)} %eq.65) | copy-start | bytes 24580
  570.0 172.0 %copy-start.11 = (s32[2048]{0:T(1024)}, s32[2048]{0:T(1024)S(1)}, u32[]{:S(2)}) copy-start(s32[2048]{0:T(1024)S(1)} %fusion.22) | copy-start | bytes 24580
  742.1 9.8 copy-start.2
  751.9 2.0 copy-start
  974.5 8.4 copy-start.17
  974.5 8.6 copy-start.8
  974.5 8.6 copy-start.12
  974.5 164.5 %copy-start.14 = (s32[2048]{0:T(1024)S(1)}, s32[2048]{0:T(1024)}, u32[]{:S(2)}) copy-start(s32[2048]{0:T(1024)} %get-tuple-element.17) | copy-start | bytes 24580
  974.5 164.5 %all-to-all-start.3 = ((bf16[16,1,192,2048]{3,2,1,0:T(8,128)(2,1)}), bf16[16,1,192,2048]{3,2,1,0:T(8,128)(2,1)}, u32[]{:S(2)}, u32[]{:S(2)}) async-start(bf16[16,1,192,2048]{3,2,1,0:T(8,128)(2,1)} %convert_bitcast_fusion), calls=%async_computation.3 | async-start | bytes 25165824 | tf_op jit(solution)/shard_map/all_to_all | solution.py:36
  1161.6 9.9 copy-start.1
  1161.6 9.9 copy-start.3
  1161.6 10.5 copy-start.4
where the time goes:
time: 1190 us; the launch traced here: 1180 us
  waiting for transfers between devices  671 us (56%)
  local copies, waits for them, and re-layouts  165 us (14%)
  blocking collectives  146 us (12%)
  matrix products  107 us (9%)
  other arithmetic  58.2 us (5%)
  starting transfers between devices  26.3 us (2%)
    ppermute x2, waiting for transfers between devices, hand_over(): lax.ppermute(lax.dynamic_slice_in_dim(down_loc, piece_idx * exp_dev, exp_...  375 us
    all_to_all x2, waiting for transfers between devices, moe_layer(): returned = lax.all_to_all(expert_out, FLAT, 0, 0, tiled=True)  296 us
    all_to_all x1, blocking collectives, moe_layer(): inbound = lax.all_to_all(outbound, FLAT, 0, 0, tiled=True)  146 us
    dot_general x2, matrix products, moe_layer(): jnp.einsum('nxcd,xdg->nxcg', inbound, layer_w13, preferred_element_type=j...  64.9 us
    gather x2, local copies, waits for them, and re-layouts, moe_layer(): jnp.take(returned.reshape(n_experts * capacity, model_width), slot_pos, a...  45 us
    dot_general x2, matrix products, moe_layer(): jnp.einsum('nxcf,xfd->nxcd', activated, layer_down, preferred_element_typ...  41.8 us
    gather x2, local copies, waits for them, and re-layouts, moe_layer(): jnp.take(normed, source_row, axis=0)  31.6 us
  transfers between devices with their start and end apart: 7, of which 4 were waited for; matrix products, arithmetic and copies ran while one was open for 7% of the time, Pallas kernels for 0%

commit v1 on v0

v1 whole, which is shorter than its diff:
```python
import functools

import jax
import jax.numpy as jnp
from jax import lax
from jax.experimental import pallas as pl
from jax.experimental.pallas import tpu as pltpu
from jax.sharding import PartitionSpec as P

NORM_EPS = 1e-6
FLAT = ("stage", "expert")
MESH = pl.DeviceIdType.MESH
F32 = jnp.float32
BF16 = jnp.bfloat16
WEIGHT_CHUNKS = 4
EARLY_PAIRS = 7


def flip(a, b):
    return a + b - 2 * a * b


def moe_kernel(tok, width, ff, w_gate, w_up, w_down, x_ref, gt_ref, w13, wdn, hid, u_all, s_loc, d2d, r1, r2, s_out, fin,
               wv_g, wv_u, wv_d, h, ub, ut, av, pp, ta, gall, gc, hs,
               wsem, lsem, gsem, us, up, ax, af, ap, az, dsend, drecv, s1, q1, s2, q2, so, hr, sw, rw):
    half = width // 2
    tile_f = min(256, ff)
    tile_d = min(256, half)
    lanes = min(128, tok)
    z = lax.axis_index("stage")
    e = lax.axis_index("expert")
    y, x, c = e // 4, (e // 2) % 2, e % 2
    me = z * 8 + e
    ny, nx, nc, nz = 1 - y, 1 - x, 1 - c, 1 - z
    fy, fx = (1 - c) * y + c * ny, (1 - c) * nx + c * x
    sy, sx = c * y + (1 - c) * ny, c * nx + (1 - c) * x

    def dev(dz, dy, dx, dc):
        return (dz, dy * 4 + dx * 2 + dc)

    def group(gz, gy, gx):
        return gz * 4 + gy * 2 + gx

    def remote(src, dst, ssem, rsem, to):
        return pltpu.make_async_remote_copy(src_ref=src, dst_ref=dst, send_sem=ssem, recv_sem=rsem, device_id=to, device_id_type=MESH)

    def local(src, dst, sem):
        cp = pltpu.make_async_copy(src, dst, sem)
        cp.start()
        cp.wait()

    own_gate = pltpu.make_async_copy(gt_ref.at[me], gall.at[me], gsem.at[2])
    own_gate.start()

    def send_gate(off, carry):
        to = lax.rem(me + off, 16)
        remote(gt_ref.at[to], gall.at[me], gsem.at[0], gsem.at[1], (to // 8, lax.rem(to, 8))).start()
        return carry

    lax.fori_loop(1, 16, send_gate, 0)

    own_x = pltpu.make_async_copy(x_ref, ub, lsem.at[0])
    own_x.start()
    w_loads = [pltpu.make_async_copy(w_gate.at[0], wv_g, wsem.at[0]), pltpu.make_async_copy(w_up.at[0], wv_u, wsem.at[1]), pltpu.make_async_copy(w_down.at[0], wv_d, wsem.at[2])]
    for load in w_loads:
        load.start()
    own_x.wait()
    h[...] = ub[...].astype(F32)

    stays = (1 - flip(z, y)) * (1 - flip(y, x)) * (1 - flip(x, c))

    def weight_parts(k, q):
        rows = pl.ds(q * (width // WEIGHT_CHUNKS), width // WEIGHT_CHUNKS)
        rows_d = pl.ds(q * (ff // WEIGHT_CHUNKS), ff // WEIGHT_CHUNKS)
        return ((w_gate.at[0, k, rows], wv_g.at[k, rows], w13.at[z, 0, rows, pl.ds(0, ff)], 0),
                (w_up.at[0, k, rows], wv_u.at[k, rows], w13.at[z, 0, rows, pl.ds(ff, ff)], 0),
                (w_down.at[0, k, rows_d], wv_d.at[k, rows_d], wdn.at[z, 0, rows_d], 1))

    def send_weights(pairs):
        for k, q in pairs:
            is_self = jnp.logical_and(stays == 1, c == k)

            @pl.when(is_self)
            def _():
                for _, src, dst, kind in weight_parts(k, q):
                    pltpu.make_async_copy(src, dst, rw.at[z, kind]).start()

            @pl.when(jnp.logical_not(is_self))
            def _():
                for src, _, dst, kind in weight_parts(k, q):
                    remote(src, dst, sw.at[k, kind], rw.at[z, kind], (y, x * 4 + c * 2 + k)).start()

    pairs = [(k, q) for q in range(WEIGHT_CHUNKS) for k in range(2)]

    def compute(k, slot, gz, gy, gx):
        g = group(gz, gy, gx)
        local(u_all.at[g], ut, lsem.at[0])
        for b in range(2):
            flat = gz * 8 + gy * 4 + gx * 2 + b
            for j in range(tok // lanes):
                row = gall[flat, :, j * lanes:(j + 1) * lanes]
                gc[b * tok + j * lanes:b * tok + (j + 1) * lanes, :] = jnp.concatenate([row] * (lanes // 8), axis=0).T
        for ex in range(2):
            def ff_tile(t, carry):
                cols = pl.ds(pl.multiple_of(t * tile_f, tile_f), tile_f)
                rows_u = ut[...].reshape(2 * tok, width)
                zg = jnp.dot(rows_u, wv_g[ex, :, cols], preferred_element_type=F32)
                zu = jnp.dot(rows_u, wv_u[ex, :, cols], preferred_element_type=F32)
                av[:, cols] = (jax.nn.silu(zg) * zu).astype(BF16)
                return carry

            lax.fori_loop(0, ff // tile_f, ff_tile, 0)

            def out_tile(t, carry):
                cols = pl.ds(pl.multiple_of(t * tile_d, tile_d), tile_d)
                side = t // (half // tile_d)
                at = pl.ds(pl.multiple_of(lax.rem(t, half // tile_d) * tile_d, tile_d), tile_d)
                o = jnp.dot(av[...], wv_d[ex, :, cols], preferred_element_type=F32).astype(BF16).astype(F32)
                gate = gc[:, ex:ex + 1]
                o = jnp.where(gate > 0, gate * o, 0.0)
                for b in range(2):
                    part = o[b * tok:(b + 1) * tok]
                    if ex:
                        part = part + pp[slot, side, b, :, at]
                    pp[slot, side, b, :, at] = part
                return carry

            lax.fori_loop(0, width // tile_d, out_tile, 0)

    def lane(gz, gy, gx):
        return u_all.at[group(gz, gy, gx), c]

    def lane_part(gz, gy, gx, which):
        return u_all.at[group(gz, gy, gx), c, pl.ds(which * (tok // 2), tok // 2)]

    def to_x(d, gz):
        return remote(lane(gz, y, x), lane(gz, y, x), ax.at[d, 0], us.at[d, 0], dev(z, y, nx, c))

    def to_y(d, gz):
        return remote(lane(gz, y, x), lane(gz, y, x), ax.at[d, 1], us.at[d, 1], dev(z, ny, x, c))

    def x_on(d, gz):
        return remote(lane_part(gz, y, nx, 0), lane_part(gz, y, nx, 0), af.at[d, 0], us.at[d, 2], dev(z, ny, x, c))

    def y_on(d, gz):
        return remote(lane_part(gz, ny, x, 1), lane_part(gz, ny, x, 1), af.at[d, 1], us.at[d, 3], dev(z, y, nx, c))

    def to_partner(d, gz, gy, gx, cls):
        return remote(lane(gz, gy, gx), lane(gz, gy, gx), ap.at[d, cls], up.at[d, cls], dev(z, y, x, nc))

    def got(dst, sem):
        pltpu.make_async_copy(dst, dst, sem).wait()

    def to_z(layer_dev):
        return remote(lane(z, y, x), lane(z, y, x), az.at[0], us.at[1, 4], dev(nz, y, x, c))

    def spread(d, gz):
        to_x(d, gz).start()
        to_y(d, gz).start()
        to_partner(d, gz, y, x, 0).start()

    def relay(d, gz):
        got(lane(gz, y, nx), us.at[d, 0])
        x_on(d, gz).start()
        to_partner(d, gz, y, nx, 1).start()
        got(lane(gz, ny, x), us.at[d, 1])
        y_on(d, gz).start()
        to_partner(d, gz, ny, x, 2).start()

    def corner(d, gz):
        got(lane_part(gz, ny, nx, 0), us.at[d, 2])
        got(lane_part(gz, ny, nx, 1), us.at[d, 3])
        to_partner(d, gz, ny, nx, 3).start()

    def d2d_copy(k, slot):
        return remote(pp.at[slot, nc], d2d.at[k], dsend.at[slot], drecv.at[k], dev(z, y, x, nc))

    def step_class(k):
        cls = k // 2
        return lax.rem(k + k // 6, 2), cls // 2, lax.rem(cls, 2)

    def first_send(k, d, ds, b):
        return remote(s_loc.at[k, b], r1.at[d * 2 + ds, b], s1.at[d * 2 + ds, b], q1.at[d * 2 + ds, b], dev(z, fy, fx, c))

    def post(k):
        slot = lax.rem(k, 2)
        d, dy, dx = step_class(k)
        df = (1 - c) * dx + c * dy
        ds = (1 - c) * dy + c * dx
        got(d2d.at[k], drecv.at[k])
        local(d2d.at[k], ta, lsem.at[0])
        for b in range(2):
            pp[slot, c, b] = pp[slot, c, b] + ta[b]
        local(pp.at[slot, c], s_loc.at[k], lsem.at[0])

        @pl.when(df == 1)
        def _():
            for b in range(2):
                first_send(k, d, ds, b).start()

    def second_send(d, b):
        return remote(s_out.at[d, b], r2.at[d, b], s2.at[d, b], q2.at[d, b], dev(z, sy, sx, c))

    def finish_second(d, b):
        k = (2 - c) * 2 + d
        load = pltpu.make_async_copy(s_loc.at[k, b], ta.at[0], lsem.at[0])
        load.start()
        got(r1.at[d * 2 + 1, b], q1.at[d * 2 + 1, b])
        local(r1.at[d * 2 + 1, b], ta.at[1], lsem.at[1])
        load.wait()
        ta[0] = ta[0] + ta[1]
        local(ta.at[0], s_out.at[d, b], lsem.at[0])
        second_send(d, b).start()

    def home_send(d, b):
        return remote(fin.at[d, b], hs.at[z, c], so.at[d, b], hr.at[z, c], dev(flip(z, d), y, x, b))

    def finish_own(d, b):
        load = pltpu.make_async_copy(s_loc.at[d, b], ta.at[0], lsem.at[0])
        load.start()
        got(r1.at[d * 2, b], q1.at[d * 2, b])
        local(r1.at[d * 2, b], ta.at[1], lsem.at[1])
        load.wait()
        ta[0] = ta[0] + ta[1]
        got(r2.at[d, b], q2.at[d, b])
        local(r2.at[d, b], ta.at[1], lsem.at[1])
        ta[0] = ta[0] + ta[1]
        local(ta.at[0], fin.at[d, b], lsem.at[0])
        if d == 1:
            home_send(d, b).start()
        else:
            @pl.when(c == b)
            def _():
                pltpu.make_async_copy(fin.at[d, b], hs.at[z, c], hr.at[z, c]).start()

            @pl.when(c != b)
            def _():
                home_send(d, b).start()

    def active():
        spread(0, z)

        @pl.when(z == 0)
        def _():
            for load in w_loads:
                load.wait()

        own_gate.wait()
        got(gall.at[pl.ds(0, 15)], gsem.at[1])

        def step(k, carry):
            d, dy, dx = step_class(k)
            gz, gy, gx = flip(z, d), flip(y, dy), flip(x, dx)
            cls = k // 2
            slot = lax.rem(k, 2)

            @pl.when(k == 1)
            def _():
                got(lane(nz, y, x), us.at[1, 4])
                spread(1, nz)

            @pl.when(k == 2)
            def _():
                relay(0, z)

            @pl.when(k == 3)
            def _():
                relay(1, nz)

            @pl.when(k == 4)
            def _():
                corner(0, z)

            @pl.when(k == 5)
            def _():
                corner(1, nz)

            got(u_all.at[group(gz, gy, gx), nc], up.at[d, cls])

            @pl.when(k >= 2)
            def _():
                d2d_copy(k - 2, slot).wait_send()

            compute(k, slot, gz, gy, gx)
            d2d_copy(k, slot).start()

            @pl.when(k >= 1)
            def _():
                post(k - 1)

            return carry

        lax.fori_loop(0, 8, step, 0)
        post(7)
        for d in (1, 0):
            for b in range(2):
                finish_second(d, b)
        for d in (1, 0):
            for b in range(2):
                finish_own(d, b)

    def drain():
        for d in range(2):
            gz = flip(z, d)
            to_x(d, gz).wait_send()
            to_y(d, gz).wait_send()
            x_on(d, gz).wait_send()
            y_on(d, gz).wait_send()
            for cls in range(4):
                to_partner(d, gz, flip(y, cls // 2), flip(x, cls % 2), cls).wait_send()
            d2d_copy(6 + d, d).wait_send()
            for b in range(2):
                for ds in range(2):
                    first_send(0, d, ds, b).wait_send()
                second_send(d, b).wait_send()
            for b in range(2):
                if d == 1:
                    home_send(d, b).wait_send()
                else:
                    @pl.when(c != b)
                    def _():
                        home_send(d, b).wait_send()

    def layer(l, carry):
        rows = min(32, tok)

        def norm(i, cc):
            r = pl.ds(pl.multiple_of(i * rows, rows), rows)
            v = h[r, :]
            ub[r, :] = (v * lax.rsqrt(jnp.mean(v * v, axis=-1, keepdims=True) + NORM_EPS)).astype(BF16)
            return cc

        lax.fori_loop(0, tok // rows, norm, 0)
        local(ub, lane(z, y, x), lsem.at[0])

        @pl.when(z != l)
        def _():
            to_z(l).start()

            @pl.when(z == 1)
            def _():
                for load in w_loads:
                    load.wait()
                send_weights(pairs[:EARLY_PAIRS])

            @pl.when(z == 0)
            def _():
                send_weights(pairs)

        @pl.when(z == l)
        def _():
            active()

            @pl.when(z == 1)
            def _():
                send_weights(pairs[EARLY_PAIRS:])

        for s in range(2):
            got(hs.at[l, s], hr.at[l, s])
            h[:, s * half:(s + 1) * half] = h[:, s * half:(s + 1) * half] + hs[l, s]
        local(h, hid.at[l], lsem.at[0])

        @pl.when(z == l)
        def _():
            drain()

        @pl.when(z != l)
        def _():
            to_z(l).wait_send()

        return carry

    lax.fori_loop(0, 2, layer, 0)

    got(gt_ref.at[pl.ds(0, 15)], gsem.at[0])
    for k in range(2):
        @pl.when(jnp.logical_not(jnp.logical_and(stays == 1, c == k)))
        def _():
            got(w13.at[0], sw.at[k, 0])
            got(wdn.at[0], sw.at[k, 1])
    for s in range(2):
        got(w13.at[s], rw.at[s, 0])
        got(wdn.at[s], rw.at[s, 1])


def solution(mesh):
    n_experts = mesh.shape["stage"] * mesh.shape["expert"]

    def per_device(gate_loc, up_loc, down_loc, x_loc, ids_loc, mix_loc):
        tok, width = x_loc.shape
        ff = gate_loc.shape[-1]
        half = width // 2
        chosen = ids_loc[..., None] == jnp.arange(n_experts)
        table = jnp.sum(jnp.where(chosen, mix_loc[..., None], 0.0), axis=2)
        table = jnp.transpose(table, (0, 2, 1)).reshape(16, 2, tok)
        table = jnp.pad(table, ((0, 0), (0, 6), (0, 0)))
        hbm = pl.BlockSpec(memory_space=pl.ANY)
        sds = jax.ShapeDtypeStruct
        outs = pl.pallas_call(
            functools.partial(moe_kernel, tok, width, ff),
            out_shape=(
                sds((2, 1, width, 2 * ff), BF16), sds((2, 1, ff, width), BF16), sds((2, tok, width), F32),
                sds((8, 2, tok, width), BF16),
                sds((8, 2, tok, half), F32), sds((8, 2, tok, half), F32),
                sds((4, 2, tok, half), F32), sds((2, 2, tok, half), F32), sds((2, 2, tok, half), F32), sds((2, 2, tok, half), F32),
            ),
            in_specs=[hbm] * 5,
            out_specs=(hbm,) * 10,
            scratch_shapes=[
                pltpu.VMEM((2, width, ff), BF16), pltpu.VMEM((2, width, ff), BF16), pltpu.VMEM((2, ff, width), BF16),
                pltpu.VMEM((tok, width), F32), pltpu.VMEM((tok, width), BF16),
                pltpu.VMEM((2, tok, width), BF16), pltpu.VMEM((2 * tok, ff), BF16),
                pltpu.VMEM((2, 2, 2, tok, half), F32), pltpu.VMEM((2, tok, half), F32),
                pltpu.VMEM((16, 8, tok), F32), pltpu.VMEM((2 * tok, min(128, tok)), F32), pltpu.VMEM((2, 2, tok, half), F32),
            ] + [pltpu.SemaphoreType.DMA(s) for s in (
                (3,), (2,), (3,), (2, 5), (2, 4), (2, 2), (2, 2), (2, 4), (1,),
                (2,), (8,), (4, 2), (4, 2), (2, 2), (2, 2), (2, 2), (2, 2), (2, 2), (2, 2))],
            compiler_params=pltpu.CompilerParams(has_side_effects=True, vmem_limit_bytes=66_000_000),
        )(gate_loc, up_loc, down_loc, x_loc, table)
        return outs[0], outs[1], outs[2]

    weight_spec = P("stage", "expert")
    token_spec = P(None, FLAT)
    return jax.shard_map(per_device, mesh=mesh, in_specs=(weight_spec, weight_spec, weight_spec, P(FLAT), token_spec, token_spec), out_specs=(token_spec, token_spec, token_spec), check_vma=False)
```

time: 1190 us -> 1210 us (1.017)
  Pallas kernels: 0 us -> 1160 us
  waiting for transfers between devices: 671 us -> 0 us
  blocking collectives: 146 us -> 0 us
  local copies, waits for them, and re-layouts: 165 us -> 25.5 us
  matrix products: 107 us -> 0 us
  other arithmetic: 58.2 us -> 0.77 us
  starting transfers between devices: 26.3 us -> 0 us
    pallas_call x0 -> x1, Pallas kernels: none -> 1160 us  [per_device(): pl.pallas_call(functools.partial(moe_kernel, tok, width, ff), out_shape=(...]
    ppermute x4 -> x0, waiting for transfers between devices: 375 us -> none  [the longest x2 375 us: hand_over(): lax.ppermute(lax.dynamic_slice_in_dim(down_loc, piece_idx * exp_dev, exp_...]
    all_to_all x3 -> x0, waiting for transfers between devices: 296 us -> none  [the longest x2 296 us: moe_layer(): returned = lax.all_to_all(expert_out, FLAT, 0, 0, tiled=True)]
    all_to_all x1 -> x0, blocking collectives: 146 us -> none  [moe_layer(): inbound = lax.all_to_all(outbound, FLAT, 0, 0, tiled=True)]
    dot_general x4 -> x0, matrix products: 107 us -> none  [the longest x2 64.9 us: moe_layer(): jnp.einsum('nxcd,xdg->nxcg', inbound, layer_w13, preferred_element_type=j...]
    gather x4 -> x0, local copies, waits for them, and re-layouts: 76.7 us -> none  [the longest x2 45 us: moe_layer(): jnp.take(returned.reshape(n_experts * capacity, model_width), slot_pos, a...]
    dynamic_update_slice x4 -> x0, local copies, waits for them, and re-layouts: 26.5 us -> none  [the longest x2 16.9 us: hand_over(): lax.dynamic_update_slice_in_dim(fused_new, fused_in, from_stage * lay_sta...]
    reduce_sum x5 -> x1, other arithmetic: 21.3 us -> 0.77 us  [per_device(): table = jnp.sum(jnp.where(chosen, mix_loc[..., None], 0.0), axis=2)]
  transfers between devices with their start and end apart: 7 -> 0, of which waited for: 4 -> 0; matrix products, arithmetic and copies ran while one was open for 7% -> 0% of each run, Pallas kernels for 0% -> 0%
where the time goes in v1:
time: 1210 us; the launch traced here: 1190 us
  Pallas kernels  1160 us (96%)
  local copies, waits for them, and re-layouts  25.5 us (2%)
    pallas_call x1, Pallas kernels, per_device(): pl.pallas_call(functools.partial(moe_kernel, tok, width, ff), out_shape=(...  1160 us
    unnamed x5, local copies, waits for them, and re-layouts  24.8 us

profile of v1, /device:TPU:9, one launch (start us, length us, event | category | flops | bytes accessed | tf_op | source)
XLA Modules:
  0.0 1185.8 jit_solution(7104379424020061202)
XLA Ops:
  0.6 0.8 select_reduce_fusion
  1.4 0.7 pad.4.gt_ref
  2.1 1158.9 %shard_map.85 = (bf16[2,1,2048,2048]{3,2,1,0:T(8,128)(2,1)}, bf16[2,1,1024,2048]{3,2,1,0:T(8,128)(2,1)}, f32[2,256,2048]{2,1,0:T(8,128)}, bf16[8,2,256,2048]{3,2...) custom-call(bf16[1,2,2048,1024]{3,2,1,0:T(8,128)(2,1)} %w_gate.1, ...), custom_call_target="tpu_custom_call" | custom-call | tf_op jit(solution)/shard_map/pallas_call | solution.py:399
  1161.0 14.2 %copy.14 = bf16[2,1,2048,2048]{3,2,1,0:T(8,128)(2,1)} copy(bf16[2,1,2048,2048]{3,2,1,0:T(8,128)(2,1)} %get-tuple-element.12) | data formatting | bytes 33554432
  1175.2 0.0 copy-start
  1175.2 8.6 copy.15
  1183.8 0.0 copy-done
  1183.8 2.0 copy.16
  (1 shorter events, 0.0 us)
Async XLA Ops:
  1175.2 8.6 copy-start

commit v2 on v1

--- a/solution.py
+++ b/solution.py
@@ -13,7 +13,11 @@
 F32 = jnp.float32
 BF16 = jnp.bfloat16
 WEIGHT_CHUNKS = 4
-EARLY_PAIRS = 7
+AHEAD = 2
+EARLY_PAIRS = 8
+ORDER = ((0, 0), (0, 1), (1, 1), (1, 2), (1, 3), (0, 2), (1, 0), (0, 3))
+STEP = {group: k for k, group in enumerate(ORDER)}
+TABLE = sum((4 * d + cls) * 8 ** k for k, (d, cls) in enumerate(ORDER))
 
 
 def flip(a, b):
@@ -22,10 +26,10 @@
 
 def moe_kernel(tok, width, ff, w_gate, w_up, w_down, x_ref, gt_ref, w13, wdn, hid, u_all, s_loc, d2d, r1, r2, s_out, fin,
                wv_g, wv_u, wv_d, h, ub, ut, av, pp, ta, gall, gc, hs,
-               wsem, lsem, gsem, us, up, ax, af, ap, az, dsend, drecv, s1, q1, s2, q2, so, hr, sw, rw):
+               wsem, lsem, gsem, us, up, ax, af, ap, az, dsend, drecv, s1, q1, s2, q2, so, hr, sw, rw, plane):
     half = width // 2
-    tile_f = min(256, ff)
-    tile_d = min(256, half)
+    tile_f = min(512, ff)
+    tile_d = min(512, half)
     lanes = min(128, tok)
     z = lax.axis_index("stage")
     e = lax.axis_index("expert")
@@ -76,31 +80,53 @@
                 (w_up.at[0, k, rows], wv_u.at[k, rows], w13.at[z, 0, rows, pl.ds(ff, ff)], 0),
                 (w_down.at[0, k, rows_d], wv_d.at[k, rows_d], wdn.at[z, 0, rows_d], 1))
 
+    def stays_here(k):
+        return jnp.logical_and(stays == 1, c == k)
+
+    def weight_copies(k, q):
+        return [remote(src, dst, sw.at[k, q, i], rw.at[z, kind], (y, x * 4 + c * 2 + k))
+                for i, (src, _, dst, kind) in enumerate(weight_parts(k, q))]
+
     def send_weights(pairs):
         for k, q in pairs:
-            is_self = jnp.logical_and(stays == 1, c == k)
-
-            @pl.when(is_self)
+            @pl.when(stays_here(k))
             def _():
                 for _, src, dst, kind in weight_parts(k, q):
                     pltpu.make_async_copy(src, dst, rw.at[z, kind]).start()
 
-            @pl.when(jnp.logical_not(is_self))
-            def _():
-                for src, _, dst, kind in weight_parts(k, q):
-                    remote(src, dst, sw.at[k, kind], rw.at[z, kind], (y, x * 4 + c * 2 + k)).start()
+            @pl.when(jnp.logical_not(stays_here(k)))
+            def _():
+                for copy in weight_copies(k, q):
+                    copy.start()
+
+    def sent_weights(pairs):
+        for k, q in pairs:
+            @pl.when(jnp.logical_not(stays_here(k)))
+            def _():
+                for copy in weight_copies(k, q):
+                    copy.wait_send()
+
+    def paced_weights(pairs):
+        for i, pair in enumerate(pairs):
+            send_weights([pair])
+            if i >= AHEAD:
+                sent_weights([pairs[i - AHEAD]])
+        sent_weights(pairs[max(0, len(pairs) - AHEAD):])
 
     pairs = [(k, q) for q in range(WEIGHT_CHUNKS) for k in range(2)]
 
-    def compute(k, slot, gz, gy, gx):
-        g = group(gz, gy, gx)
-        local(u_all.at[g], ut, lsem.at[0])
+    def rows_load(gz, gy, gx):
+        return pltpu.make_async_copy(u_all.at[group(gz, gy, gx)], ut, lsem.at[2])
+
+    def gate_columns(gz, gy, gx):
         for b in range(2):
             flat = gz * 8 + gy * 4 + gx * 2 + b
             for j in range(tok // lanes):
                 row = gall[flat, :, j * lanes:(j + 1) * lanes]
                 gc[b * tok + j * lanes:b * tok + (j + 1) * lanes, :] = jnp.concatenate([row] * (lanes // 8), axis=0).T
-        for ex in range(2):
+
+    def expert(ex, slot):
+        if True:
             def ff_tile(t, carry):
                 cols = pl.ds(pl.multiple_of(t * tile_f, tile_f), tile_f)
                 rows_u = ut[...].reshape(2 * tok, width)
@@ -176,22 +202,29 @@
         return remote(pp.at[slot, nc], d2d.at[k], dsend.at[slot], drecv.at[k], dev(z, y, x, nc))
 
     def step_class(k):
-        cls = k // 2
-        return lax.rem(k + k // 6, 2), cls // 2, lax.rem(cls, 2)
+        code = lax.rem(lax.div(jnp.int32(TABLE), lax.shift_left(jnp.int32(1), 3 * k)), 8)
+        return code // 4, lax.rem(code // 2, 2), lax.rem(code, 2)
 
     def first_send(k, d, ds, b):
         return remote(s_loc.at[k, b], r1.at[d * 2 + ds, b], s1.at[d * 2 + ds, b], q1.at[d * 2 + ds, b], dev(z, fy, fx, c))
 
-    def post(k):
-        slot = lax.rem(k, 2)
+    def sum_load(k):
+        return pltpu.make_async_copy(d2d.at[k], ta, lsem.at[3])
+
+    def sum_store(k, slot):
+        return pltpu.make_async_copy(pp.at[slot, c], s_loc.at[k], lsem.at[4])
+
+    def add_partner(k, slot):
+        sum_load(k).wait()
+        for b in range(2):
+            pp[slot, c, b] = pp[slot, c, b] + ta[b]
+        sum_store(k, slot).start()
+
+    def pass_on(k, slot):
         d, dy, dx = step_class(k)
         df = (1 - c) * dx + c * dy
         ds = (1 - c) * dy + c * dx
-        got(d2d.at[k], drecv.at[k])
-        local(d2d.at[k], ta, lsem.at[0])
-        for b in range(2):
-            pp[slot, c, b] = pp[slot, c, b] + ta[b]
-        local(pp.at[slot, c], s_loc.at[k], lsem.at[0])
+        sum_store(k, slot).wait()
 
         @pl.when(df == 1)
         def _():
@@ -202,7 +235,7 @@
         return remote(s_out.at[d, b], r2.at[d, b], s2.at[d, b], q2.at[d, b], dev(z, sy, sx, c))
 
     def finish_second(d, b):
-        k = (2 - c) * 2 + d
+        k = c * STEP[d, 1] + (1 - c) * STEP[d, 2]
         load = pltpu.make_async_copy(s_loc.at[k, b], ta.at[0], lsem.at[0])
         load.start()
         got(r1.at[d * 2 + 1, b], q1.at[d * 2 + 1, b])
@@ -216,7 +249,7 @@
         return remote(fin.at[d, b], hs.at[z, c], so.at[d, b], hr.at[z, c], dev(flip(z, d), y, x, b))
 
     def finish_own(d, b):
-        load = pltpu.make_async_copy(s_loc.at[d, b], ta.at[0], lsem.at[0])
+        load = pltpu.make_async_copy(s_loc.at[STEP[d, 0], b], ta.at[0], lsem.at[0])
         load.start()
         got(r1.at[d * 2, b], q1.at[d * 2, b])
         local(r1.at[d * 2, b], ta.at[1], lsem.at[1])
@@ -251,7 +284,7 @@
         def step(k, carry):
             d, dy, dx = step_class(k)
             gz, gy, gx = flip(z, d), flip(y, dy), flip(x, dx)
-            cls = k // 2
+            cls = dy * 2 + dx
             slot = lax.rem(k, 2)
 
             @pl.when(k == 1)
@@ -259,45 +292,58 @@
                 got(lane(nz, y, x), us.at[1, 4])
                 spread(1, nz)
 
-            @pl.when(k == 2)
-            def _():
-                relay(0, z)
-
-            @pl.when(k == 3)
-            def _():
-                relay(1, nz)
-
-            @pl.when(k == 4)
-            def _():
-                corner(0, z)
-
-            @pl.when(k == 5)
-            def _():
-                corner(1, nz)
+            for dd in range(2):
+                @pl.when(k == max(1, min(STEP[dd, 1], STEP[dd, 2])))
+                def _():
+                    relay(dd, flip(z, dd))
+
+                @pl.when(k == STEP[dd, 3])
+                def _():
+                    corner(dd, flip(z, dd))
 
             got(u_all.at[group(gz, gy, gx), nc], up.at[d, cls])
+            rows_load(gz, gy, gx).start()
+            gate_columns(gz, gy, gx)
 
             @pl.when(k >= 2)
             def _():
+                pass_on(k - 2, slot)
                 d2d_copy(k - 2, slot).wait_send()
 
-            compute(k, slot, gz, gy, gx)
+            rows_load(gz, gy, gx).wait()
+            expert(0, slot)
+
+            @pl.when(k == 7)
+            def _():
+                for b in range(2):
+                    finish_second(1, b)
+
+            @pl.when(k >= 1)
+            def _():
+                got(d2d.at[k - 1], drecv.at[k - 1])
+                sum_load(k - 1).start()
+
+            expert(1, slot)
+
+            @pl.when(k >= 1)
+            def _():
+                add_partner(k - 1, 1 - slot)
+
             d2d_copy(k, slot).start()
-
-            @pl.when(k >= 1)
-            def _():
-                post(k - 1)
-
             return carry
 
         lax.fori_loop(0, 8, step, 0)
-        post(7)
-        for d in (1, 0):
-            for b in range(2):
-                finish_second(d, b)
-        for d in (1, 0):
-            for b in range(2):
-                finish_own(d, b)
+        pass_on(6, 0)
+        got(d2d.at[7], drecv.at[7])
+        sum_load(7).start()
+        add_partner(7, 1)
+        pass_on(7, 1)
+        for b in range(2):
+            finish_own(1, b)
+        for b in range(2):
+            finish_second(0, b)
+        for b in range(2):
+            finish_own(0, b)
 
     def drain():
         for d in range(2):
@@ -336,6 +382,10 @@
         @pl.when(z != l)
         def _():
             to_z(l).start()
+            to_z(l).wait_send()
+            for i in range(1, 8):
+                pl.semaphore_signal(plane, inc=1, device_id=(z, lax.rem(e + i, 8)), device_id_type=MESH)
+            pl.semaphore_wait(plane, 7)
 
             @pl.when(z == 1)
             def _():
@@ -364,20 +414,19 @@
         def _():
             drain()
 
-        @pl.when(z != l)
-        def _():
-            to_z(l).wait_send()
-
         return carry
 
     lax.fori_loop(0, 2, layer, 0)
 
     got(gt_ref.at[pl.ds(0, 15)], gsem.at[0])
-    for k in range(2):
-        @pl.when(jnp.logical_not(jnp.logical_and(stays == 1, c == k)))
-        def _():
-            got(w13.at[0], sw.at[k, 0])
-            got(wdn.at[0], sw.at[k, 1])
+    @pl.when(z == 0)
+    def _():
+        sent_weights(pairs)
+
+    @pl.when(z == 1)
+    def _():
+        sent_weights(pairs)
+
     for s in range(2):
         got(w13.at[s], rw.at[s, 0])
         got(wdn.at[s], rw.at[s, 1])
@@ -413,8 +462,8 @@
                 pltpu.VMEM((2, 2, 2, tok, half), F32), pltpu.VMEM((2, tok, half), F32),
                 pltpu.VMEM((16, 8, tok), F32), pltpu.VMEM((2 * tok, min(128, tok)), F32), pltpu.VMEM((2, 2, tok, half), F32),
             ] + [pltpu.SemaphoreType.DMA(s) for s in (
-                (3,), (2,), (3,), (2, 5), (2, 4), (2, 2), (2, 2), (2, 4), (1,),
-                (2,), (8,), (4, 2), (4, 2), (2, 2), (2, 2), (2, 2), (2, 2), (2, 2), (2, 2))],
+                (3,), (5,), (3,), (2, 5), (2, 4), (2, 2), (2, 2), (2, 4), (1,),
+                (2,), (8,), (4, 2), (4, 2), (2, 2), (2, 2), (2, 2), (2, 2), (2, WEIGHT_CHUNKS, 3), (2, 2))] + [pltpu.SemaphoreType.REGULAR],
             compiler_params=pltpu.CompilerParams(has_side_effects=True, vmem_limit_bytes=66_000_000),
         )(gate_loc, up_loc, down_loc, x_loc, table)
         return outs[0], outs[1], outs[2]

time: 1210 us -> 606 us (0.50); the launches traced: 1190 us -> 605 us
  Pallas kernels: 1160 us -> 578 us
    pallas_call x1, Pallas kernels: 1160 us -> 578 us  [per_device(): pl.pallas_call(functools.partial(moe_kernel, tok, width, ff), out_shape=(...]
where the time goes in v2:
time: 606 us; the launch traced here: 605 us
  Pallas kernels  578 us (95%)
  local copies, waits for them, and re-layouts  25.5 us (4%)
    pallas_call x1, Pallas kernels, per_device(): pl.pallas_call(functools.partial(moe_kernel, tok, width, ff), out_shape=(...  578 us
    unnamed x5, local copies, waits for them, and re-layouts  24.8 us

profile of v2, /device:TPU:9, one launch (start us, length us, event | category | flops | bytes accessed | tf_op | source)
XLA Modules:
  0.0 605.1 jit_solution(12997573316677314854)
XLA Ops:
  0.6 0.8 select_reduce_fusion
  1.4 0.7 pad.4.gt_ref
  2.1 578.2 %shard_map.85 = (bf16[2,1,2048,2048]{3,2,1,0:T(8,128)(2,1)}, bf16[2,1,1024,2048]{3,2,1,0:T(8,128)(2,1)}, f32[2,256,2048]{2,1,0:T(8,128)}, bf16[8,2,256,2048]{3,2...) custom-call(bf16[1,2,2048,1024]{3,2,1,0:T(8,128)(2,1)} %w_gate.1, ...), custom_call_target="tpu_custom_call" | custom-call | tf_op jit(solution)/shard_map/pallas_call | solution.py:448
  580.3 14.2 %copy.14 = bf16[2,1,2048,2048]{3,2,1,0:T(8,128)(2,1)} copy(bf16[2,1,2048,2048]{3,2,1,0:T(8,128)(2,1)} %get-tuple-element.12) | data formatting | bytes 33554432
  594.5 0.0 copy-start
  594.5 8.6 %copy.15 = bf16[2,1,1024,2048]{3,2,1,0:T(8,128)(2,1)} copy(bf16[2,1,1024,2048]{3,2,1,0:T(8,128)(2,1)} %get-tuple-element.13) | data formatting | bytes 16777216
  603.1 0.0 copy-done
  603.1 2.0 copy.16
  (1 shorter events, 0.0 us)
Async XLA Ops:
  594.5 8.6 %copy-start = (f32[2,256,2048]{2,1,0:T(8,128)S(1)}, f32[2,256,2048]{2,1,0:T(8,128)}, u32[]{:S(2)}) copy-start(f32[2,256,2048]{2,1,0:T(8,128)} %get-tuple-element.14) | copy-start | bytes 12582916

commit v3 on v2

--- a/solution.py
+++ b/solution.py
@@ -12,10 +12,11 @@
 MESH = pl.DeviceIdType.MESH
 F32 = jnp.float32
 BF16 = jnp.bfloat16
-WEIGHT_CHUNKS = 4
-AHEAD = 2
-EARLY_PAIRS = 8
-ORDER = ((0, 0), (0, 1), (1, 1), (1, 2), (1, 3), (0, 2), (1, 0), (0, 3))
+WEIGHT_CHUNKS = 8
+COPY_STEPS = 8
+GAPS_STAY = (2,)
+GAPS_LEAVE = (2, 3)
+ORDER = ((0, 0), (0, 1), (1, 1), (1, 3), (1, 2), (0, 3), (0, 2), (1, 0))
 STEP = {group: k for k, group in enumerate(ORDER)}
 TABLE = sum((4 * d + cls) * 8 ** k for k, (d, cls) in enumerate(ORDER))
 
@@ -28,8 +29,8 @@
                wv_g, wv_u, wv_d, h, ub, ut, av, pp, ta, gall, gc, hs,
                wsem, lsem, gsem, us, up, ax, af, ap, az, dsend, drecv, s1, q1, s2, q2, so, hr, sw, rw, plane):
     half = width // 2
-    tile_f = min(512, ff)
-    tile_d = min(512, half)
+    tile_f = min(1024, ff)
+    tile_d = min(1024, half)
     lanes = min(128, tok)
     z = lax.axis_index("stage")
     e = lax.axis_index("expert")
@@ -66,9 +67,9 @@
     own_x = pltpu.make_async_copy(x_ref, ub, lsem.at[0])
     own_x.start()
     w_loads = [pltpu.make_async_copy(w_gate.at[0], wv_g, wsem.at[0]), pltpu.make_async_copy(w_up.at[0], wv_u, wsem.at[1]), pltpu.make_async_copy(w_down.at[0], wv_d, wsem.at[2])]
+    own_x.wait()
     for load in w_loads:
         load.start()
-    own_x.wait()
     h[...] = ub[...].astype(F32)
 
     stays = (1 - flip(z, y)) * (1 - flip(y, x)) * (1 - flip(x, c))
@@ -106,14 +107,8 @@
                 for copy in weight_copies(k, q):
                     copy.wait_send()
 
-    def paced_weights(pairs):
-        for i, pair in enumerate(pairs):
-            send_weights([pair])
-            if i >= AHEAD:
-                sent_weights([pairs[i - AHEAD]])
-        sent_weights(pairs[max(0, len(pairs) - AHEAD):])
-
     pairs = [(k, q) for q in range(WEIGHT_CHUNKS) for k in range(2)]
+    leaves = flip(y, z) == 1
 
     def rows_load(gz, gy, gx):
         return pltpu.make_async_copy(u_all.at[group(gz, gy, gx)], ut, lsem.at[2])
@@ -300,6 +295,12 @@
                 @pl.when(k == STEP[dd, 3])
                 def _():
                     corner(dd, flip(z, dd))
+
+            for mine, gaps in ((jnp.logical_not(leaves), GAPS_STAY), (leaves, GAPS_LEAVE)):
+                for pair, at in zip(pairs, gaps):
+                    @pl.when(jnp.logical_and(mine, k == at))
+                    def _():
+                        send_weights([pair])
 
             got(u_all.at[group(gz, gy, gx), nc], up.at[d, cls])
             rows_load(gz, gy, gx).start()
@@ -382,28 +383,28 @@
         @pl.when(z != l)
         def _():
             to_z(l).start()
+
+            @pl.when(z == 1)
+            def _():
+                for load in w_loads:
+                    load.wait()
+
+            @pl.when(jnp.logical_not(leaves))
+            def _():
+                send_weights(pairs[len(GAPS_STAY):])
+
             to_z(l).wait_send()
             for i in range(1, 8):
                 pl.semaphore_signal(plane, inc=1, device_id=(z, lax.rem(e + i, 8)), device_id_type=MESH)
             pl.semaphore_wait(plane, 7)
 
-            @pl.when(z == 1)
-            def _():
-                for load in w_loads:
-                    load.wait()
-                send_weights(pairs[:EARLY_PAIRS])
-
-            @pl.when(z == 0)
-            def _():
-                send_weights(pairs)
+            @pl.when(leaves)
+            def _():
+                send_weights(pairs[len(GAPS_LEAVE):])
 
         @pl.when(z == l)
         def _():
             active()
-
-            @pl.when(z == 1)
-            def _():
-                send_weights(pairs[EARLY_PAIRS:])
 
         for s in range(2):
             got(hs.at[l, s], hr.at[l, s])
@@ -419,17 +420,29 @@
     lax.fori_loop(0, 2, layer, 0)
 
     got(gt_ref.at[pl.ds(0, 15)], gsem.at[0])
-    @pl.when(z == 0)
-    def _():
-        sent_weights(pairs)
-
-    @pl.when(z == 1)
-    def _():
-        sent_weights(pairs)
-
+    sent_weights(pairs)
     for s in range(2):
         got(w13.at[s], rw.at[s, 0])
         got(wdn.at[s], rw.at[s, 1])
+
+
+def copy_blocks(*refs):
+    for src, dst in zip(refs[:3], refs[3:]):
+        dst[...] = src[...]
+
+
+def hand_out(arrays):
+    flat = [a.reshape(-1, a.shape[-1]) for a in arrays]
+    specs = [pl.BlockSpec((a.shape[0] // COPY_STEPS, a.shape[1]), lambda i: (i, 0)) for a in flat]
+    outs = pl.pallas_call(
+        copy_blocks,
+        grid=(COPY_STEPS,),
+        out_shape=[jax.ShapeDtypeStruct(a.shape, a.dtype) for a in flat],
+        in_specs=specs,
+        out_specs=specs,
+        compiler_params=pltpu.CompilerParams(vmem_limit_bytes=48_000_000),
+    )(*flat)
+    return tuple(o.reshape(a.shape) for o, a in zip(outs, arrays))
 
 
 def solution(mesh):
@@ -466,7 +479,7 @@
                 (2,), (8,), (4, 2), (4, 2), (2, 2), (2, 2), (2, 2), (2, 2), (2, WEIGHT_CHUNKS, 3), (2, 2))] + [pltpu.SemaphoreType.REGULAR],
             compiler_params=pltpu.CompilerParams(has_side_effects=True, vmem_limit_bytes=66_000_000),
         )(gate_loc, up_loc, down_loc, x_loc, table)
-        return outs[0], outs[1], outs[2]
+        return hand_out(outs[:3])
 
     weight_spec = P("stage", "expert")
     token_spec = P(None, FLAT)

time: 606 us -> 561 us (0.926)
  local copies, waits for them, and re-layouts: 25.5 us -> 2.87 us
  Pallas kernels: 578 us -> 556 us
    pallas_call x1, Pallas kernels: 578 us -> 537 us  [per_device(): pl.pallas_call(functools.partial(moe_kernel, tok, width, ff), out_shape=(...]
    unnamed x5 -> x2, local copies, waits for them, and re-layouts: 24.8 us -> 2.18 us
    pallas_call x0 -> x1, Pallas kernels: none -> 18.7 us  [hand_out(): pl.pallas_call(copy_blocks, grid=(COPY_STEPS,), out_shape=[jax.ShapeDtype...]
where the time goes in v3:
time: 561 us; the launch traced here: 560 us
  Pallas kernels  556 us (99%)
    pallas_call x1, Pallas kernels, per_device(): pl.pallas_call(functools.partial(moe_kernel, tok, width, ff), out_shape=(...  537 us
    pallas_call x1, Pallas kernels, hand_out(): pl.pallas_call(copy_blocks, grid=(COPY_STEPS,), out_shape=[jax.ShapeDtype...  18.7 us

profile of v3, /device:TPU:9, one launch (start us, length us, event | category | flops | bytes accessed | tf_op | source)
XLA Modules:
  0.0 560.4 jit_solution(7316408022653279208)
XLA Ops:
  0.6 0.8 select_reduce_fusion
  1.4 0.7 pad.4.gt_ref
  2.1 537.4 %shard_map.85 = (bf16[2,1,2048,2048]{3,2,1,0:T(8,128)(2,1)}, bf16[2,1,1024,2048]{3,2,1,0:T(8,128)(2,1)}, f32[2,256,2048]{2,1,0:T(8,128)}, bf16[8,2,256,2048]{3,2...) custom-call(bf16[1,2,2048,1024]{3,2,1,0:T(8,128)(2,1)} %w_gate.1, ...), custom_call_target="tpu_custom_call" | custom-call | tf_op jit(solution)/shard_map/pallas_call | solution.py:461
  539.5 0.0 copy-start
  539.5 2.2 copy-done
  541.7 18.7 %shard_map.86 = (bf16[4096,2048]{1,0:T(8,128)(2,1)}, bf16[2048,2048]{1,0:T(8,128)(2,1)}, f32[512,2048]{1,0:T(8,128)}) custom-call(bf16[4096,2048]{1,0:T(8,128)(2,1)} %bitcast.12, bf16[2048,2048]{1,0:T(8,128)(2,1)} %bitcast.13, f32[512,2048]{1,0:T(8,128)S(1)} %bitcast.11), custom_call_target="tpu_custom_call" | custom-call | tf_op jit(solution)/shard_map/pallas_call | solution.py:437
  (1 shorter events, 0.0 us)
Async XLA Ops:
  539.5 2.2 copy-start

commit v4 on v3

--- a/solution.py
+++ b/solution.py
@@ -13,7 +13,7 @@
 F32 = jnp.float32
 BF16 = jnp.bfloat16
 WEIGHT_CHUNKS = 8
-COPY_STEPS = 8
+COPY_STEPS = 4
 GAPS_STAY = (2,)
 GAPS_LEAVE = (2, 3)
 ORDER = ((0, 0), (0, 1), (1, 1), (1, 3), (1, 2), (0, 3), (0, 2), (1, 0))
@@ -340,9 +340,9 @@
         add_partner(7, 1)
         pass_on(7, 1)
         for b in range(2):
+            finish_second(0, b)
+        for b in range(2):
             finish_own(1, b)
-        for b in range(2):
-            finish_second(0, b)
         for b in range(2):
             finish_own(0, b)
 

time: 561 us -> 559 us (level)
  no operation moved by 1% of the time
where the time goes in v4:
time: 559 us
  Pallas kernels  554 us (99%)
    pallas_call x1, Pallas kernels, per_device(): pl.pallas_call(functools.partial(moe_kernel, tok, width, ff), out_shape=(...  537 us
    pallas_call x1, Pallas kernels, hand_out(): pl.pallas_call(copy_blocks, grid=(COPY_STEPS,), out_shape=[jax.ShapeDtype...  17.4 us

profile of v4, /device:TPU:9, one launch (start us, length us, event | category | flops | bytes accessed | tf_op | source)
XLA Modules:
  0.0 558.5 jit_solution(5121316666180854400)
XLA Ops:
  0.6 0.8 select_reduce_fusion
  1.4 0.7 pad.4.gt_ref
  2.1 536.8 %shard_map.85 = (bf16[2,1,2048,2048]{3,2,1,0:T(8,128)(2,1)}, bf16[2,1,1024,2048]{3,2,1,0:T(8,128)(2,1)}, f32[2,256,2048]{2,1,0:T(8,128)}, bf16[8,2,256,2048]{3,2...) custom-call(bf16[1,2,2048,1024]{3,2,1,0:T(8,128)(2,1)} %w_gate.1, ...), custom_call_target="tpu_custom_call" | custom-call | tf_op jit(solution)/shard_map/pallas_call | solution.py:461
  538.9 0.0 copy-start
  538.9 2.2 copy-done
  541.1 17.4 %shard_map.86 = (bf16[4096,2048]{1,0:T(8,128)(2,1)}, bf16[2048,2048]{1,0:T(8,128)(2,1)}, f32[512,2048]{1,0:T(8,128)}) custom-call(bf16[4096,2048]{1,0:T(8,128)(2,1)} %bitcast.12, bf16[2048,2048]{1,0:T(8,128)(2,1)} %bitcast.13, f32[512,2048]{1,0:T(8,128)S(1)} %bitcast.11), custom_call_target="tpu_custom_call" | custom-call | tf_op jit(solution)/shard_map/pallas_call | solution.py:437
  (1 shorter events, 0.0 us)
Async XLA Ops:
  538.9 2.2 copy-start
